TPU v7x, 32 devices: a whole 2x2x4 slice. The times are simulated.
32 devices in a mesh: rep: 1, dp: 32 (over x, y, z, core).
Axes of the slice: x: 2, y: 2, z: 4, core: 2. Of those that a mesh axis runs over, the one named last changes fastest.
Arguments:
- g_w_gate: bfloat16 [32, 2, 1024, 2816], P(('rep', 'dp'))
- g_w_up: bfloat16 [32, 2, 1024, 2816], P(('rep', 'dp'))
- g_w_down: bfloat16 [32, 2, 2816, 1024], P(('rep', 'dp'))
- w_gate: bfloat16 [2, 1024, 2816], replicated
- w_up: bfloat16 [2, 1024, 2816], replicated
- w_down: bfloat16 [2, 2816, 1024], replicated
- m_w_gate: float32 [2, 1024, 2816], P(None, 'dp')
- m_w_up: float32 [2, 1024, 2816], P(None, 'dp')
- m_w_down: float32 [2, 2816, 1024], P(None, 'dp')
- v_w_gate: float32 [2, 1024, 2816], P(None, 'dp')
- v_w_up: float32 [2, 1024, 2816], P(None, 'dp')
- v_w_down: float32 [2, 2816, 1024], P(None, 'dp')
Outputs:
- output 1: bfloat16 [2, 1024, 2816], P('rep')
- output 2: bfloat16 [2, 1024, 2816], P('rep')
- output 3: bfloat16 [2, 2816, 1024], P('rep')
- output 4: float32 [2, 1024, 2816], P('rep', 'dp')
- output 5: float32 [2, 1024, 2816], P('rep', 'dp')
- output 6: float32 [2, 2816, 1024], P('rep', 'dp')
- output 7: float32 [2, 1024, 2816], P('rep', 'dp')
- output 8: float32 [2, 1024, 2816], P('rep', 'dp')
- output 9: float32 [2, 2816, 1024], P('rep', 'dp')
All inputs are finite; a program needn't handle non-finite values.
Results may differ from a plain program's by a relative error of at most 0.022.
Values are sent between devices in bfloat16 or wider.
A program may use at most 2 GiB of HBM per device.

v0:
```python
import jax
import jax.numpy as jnp
from jax import lax
from jax.sharding import PartitionSpec as P


def adamw(w, m, v, g):
    m = 0.9 * m + 0.1 * g
    v = 0.95 * v + 0.05 * g * g
    step = m * lax.rsqrt(v + 1e-8) + 0.1 * w
    return (w - 0.02 * step).astype(jnp.bfloat16), m, v


def solution(mesh):
    def step(*arrays):
        terms, weights, m, v = (arrays[i : i + 3] for i in (0, 3, 6, 9))
        gradients = [lax.psum_scatter(t[0], "dp", scatter_dimension=1, tiled=True).astype(jnp.float32) for t in terms]
        me = lax.axis_index("dp")
        own = [lax.dynamic_slice_in_dim(w, me * one.shape[1], one.shape[1], 1).astype(jnp.float32) for w, one in zip(weights, m, strict=True)]
        new = [adamw(w, m, v, g) for w, m, v, g in zip(own, m, v, gradients, strict=True)]
        whole = [lax.all_gather(one[0], "dp", axis=1, tiled=True) for one in new]
        return (*whole, *(one[1] for one in new), *(one[2] for one in new))

    all_of, cut = P(None, None, None), P(None, "dp", None)
    return jax.shard_map(
        step,
        mesh=mesh,
        in_specs=(P(("rep", "dp"), None, None, None),) * 3 + (all_of,) * 3 + (cut,) * 6,
        out_specs=(P("rep", None, None),) * 3 + (P("rep", "dp", None),) * 6,
        check_vma=False,
    )
```

profile of v0, /device:TPU:0, one launch (start us, length us, event | category | flops | bytes accessed | tf_op | source)
XLA Modules:
  0.0 803.7 jit_solution(5705674072012351525)
XLA Ops:
  7.2 0.0 reduce-scatter.8.cloned.1.call-start
  7.2 0.7 reduce-scatter.8.cloned.1.call-update
  7.9 0.0 reduce-scatter.6.cloned.1.call-start
  8.0 0.7 reduce-scatter.6.cloned.1.call-update
  8.7 0.0 reduce-scatter.10.cloned.1.call-start
  8.7 19.6 %copy.21 = bf16[2,2816,1024]{2,0,1:T(2,128)(2,1)S(1)} copy(bf16[2,2816,1024]{2,1,0:T(8,128)(2,1)} %bitcast.9) | data formatting | bytes 23068672
  28.3 6.5 copy.23
  34.8 0.0 copy-start.1
  34.8 0.0 copy-start.2
  34.8 0.0 copy-start.3
  34.8 0.0 copy-start.4
  34.8 0.0 reduce-scatter.10.cloned.1.call-update
  34.9 0.0 all-gather.6.cloned.1.call-start
  34.9 138.4 %reduce-scatter.8.cloned.1.call-done = bf16[2,32,2816]{2,1,0:T(8,128)(2,1)} async-done(((bf16[2,1024,2816]{2,1,0:T(8,128)(2,1)}), bf16[2,32,2816]{2,1,0:T(8,128)(2,1)}) %reduce-scatter.8.cloned.1.call-update) | async-done | bytes 360464 | tf_op jit(solution)/shard_map/reduce_scatter | solution.py:17
  173.3 0.0 copy-done.1
  173.3 0.0 copy-done.2
  173.3 2.5 fusion.6
  175.8 0.0 all-gather.6.cloned.1.call-update
  175.8 0.0 all-gather.4.cloned.1.call-start
  175.9 158.0 %reduce-scatter.6.cloned.1.call-done = bf16[2,32,2816]{2,1,0:T(8,128)(2,1)} async-done(((bf16[2,1024,2816]{2,1,0:T(8,128)(2,1)}), bf16[2,32,2816]{2,1,0:T(8,128)(2,1)}) %reduce-scatter.6.cloned.1.call-update) | async-done | bytes 360464 | tf_op jit(solution)/shard_map/reduce_scatter | solution.py:17
  333.8 0.0 copy-done.3
  333.8 0.0 copy-done.4
  333.9 2.5 fusion.2
  336.3 0.0 all-gather.4.cloned.1.call-update
  336.3 0.0 all-gather.8.cloned.1.call-start
  336.4 158.5 %reduce-scatter.10.cloned.1.call-done = bf16[88,2048]{1,0:T(8,128)(2,1)} async-done(((bf16[2816,2048]{1,0:T(8,128)(2,1)}), bf16[88,2048]{1,0:T(8,128)(2,1)}) %reduce-scatter.10.cloned.1.call-update) | async-done | bytes 360464
  494.9 1.2 reshape.19
  496.1 2.9 fusion.10
  499.0 0.0 all-gather.8.cloned.1.call-update
  499.1 88.0 %all-gather.6.cloned.1.call-done = bf16[2,1024,2816]{2,1,0:T(8,128)(2,1)} async-done(((bf16[2,32,2816]{2,1,0:T(8,128)(2,1)}), bf16[2,1024,2816]{2,1,0:T(8,128)(2,1)}) %all-gather.6.cloned.1.call-update) | async-done | bytes 11534352 | tf_op jit(solution)/shard_map/all_gather | solution.py:21
  587.1 92.9 %all-gather.4.cloned.1.call-done = bf16[2,1024,2816]{2,1,0:T(8,128)(2,1)} async-done(((bf16[2,32,2816]{2,1,0:T(8,128)(2,1)}), bf16[2,1024,2816]{2,1,0:T(8,128)(2,1)}) %all-gather.4.cloned.1.call-update) | async-done | bytes 11534352 | tf_op jit(solution)/shard_map/all_gather | solution.py:21
  680.0 92.9 %all-gather.8.cloned.1.call-done = bf16[2,2816,1024]{2,1,0:T(8,128)(2,1)} async-done(((bf16[2,88,1024]{2,1,0:T(8,128)(2,1)}), bf16[2,2816,1024]{2,1,0:T(8,128)(2,1)}) %all-gather.8.cloned.1.call-update) | async-done | bytes 11534352 | tf_op jit(solution)/shard_map/all_gather | solution.py:21
  772.8 0.0 copy-start
  772.9 0.0 slice-start
  772.9 0.0 slice-start.1
  772.9 11.7 %copy.31 = bf16[2,1024,2816]{2,1,0:T(8,128)(2,1)} copy(bf16[2,1024,2816]{2,1,0:T(8,128)(2,1)} %all-gather.4.cloned.1.call-done) | data formatting | bytes 23068672
  784.5 0.0 copy-done
  784.5 0.0 slice-start.2
  784.5 5.8 copy.32
  790.4 0.0 slice-done
  790.4 0.8 slice-done.1
  791.1 1.2 slice-done.2
  792.4 4.4 copy.33
  (1 shorter events, 0.0 us)
Async XLA Ops:
  7.2 166.1 %reduce-scatter.8.cloned.1.call-start = ((), (), s32[]{:S(2)}) async-start(), calls=%async_computation.5 | async-start | bytes 11894784 | tf_op jit(solution)/shard_map/reduce_scatter | solution.py:17
  7.9 325.9 %reduce-scatter.6.cloned.1.call-start = ((), (), s32[]{:S(2)}) async-start(), calls=%async_computation.3 | async-start | bytes 11894784 | tf_op jit(solution)/shard_map/reduce_scatter | solution.py:17
  8.7 486.2 %reduce-scatter.10.cloned.1.call-start = ((), (), s32[]{:S(2)}) async-start(), calls=%async_computation.8 | async-start | bytes 11894784
  34.8 138.5 %copy-start.1 = (f32[2,32,2816]{2,1,0:T(8,128)S(1)}, f32[2,32,2816]{2,1,0:T(8,128)}, u32[]{:S(2)}) copy-start(f32[2,32,2816]{2,1,0:T(8,128)} %param.22) | copy-start | bytes 2162692
  34.8 138.5 %copy-start.2 = (f32[2,32,2816]{2,1,0:T(8,128)S(1)}, f32[2,32,2816]{2,1,0:T(8,128)}, u32[]{:S(2)}) copy-start(f32[2,32,2816]{2,1,0:T(8,128)} %param.19) | copy-start | bytes 2162692
  34.8 299.0 %copy-start.3 = (f32[2,32,2816]{2,1,0:T(8,128)S(1)}, f32[2,32,2816]{2,1,0:T(8,128)}, u32[]{:S(2)}) copy-start(f32[2,32,2816]{2,1,0:T(8,128)} %param.21) | copy-start | bytes 2162692
  34.8 299.0 %copy-start.4 = (f32[2,32,2816]{2,1,0:T(8,128)S(1)}, f32[2,32,2816]{2,1,0:T(8,128)}, u32[]{:S(2)}) copy-start(f32[2,32,2816]{2,1,0:T(8,128)} %param.18) | copy-start | bytes 2162692
  34.9 552.2 %all-gather.6.cloned.1.call-start = ((), (), s32[]{:S(2)}) async-start(), calls=%async_computation.6 | async-start | bytes 11894784 | tf_op jit(solution)/shard_map/all_gather | solution.py:21
  175.8 504.1 %all-gather.4.cloned.1.call-start = ((), (), s32[]{:S(2)}) async-start(), calls=%async_computation.4 | async-start | bytes 11894784 | tf_op jit(solution)/shard_map/all_gather | solution.py:21
  336.3 436.5 %all-gather.8.cloned.1.call-start = ((), (), s32[]{:S(2)}) async-start(), calls=%async_computation.7 | async-start | bytes 11894784 | tf_op jit(solution)/shard_map/all_gather | solution.py:21
  772.8 11.7 %copy-start = (bf16[2,1024,2816]{2,1,0:T(8,128)(2,1)S(1)}, bf16[2,1024,2816]{2,1,0:T(8,128)(2,1)}, u32[]{:S(2)}) copy-start(bf16[2,1024,2816]{2,1,0:T(8,128)(2,1)} %all-gather.6.cloned.1.call-done) | copy-start | bytes 34603012
  772.9 17.5 %slice-start = ((s8[11534336]{0:T(1024)(128)(4,1)}), s8[4194304]{0:T(1024)(128)(4,1)S(1)}, s32[]{:S(2)}) async-start(s8[11534336]{0:T(1024)(128)(4,1)} %bitcast.12), calls=%async_computation.9 | async-start | bytes 8388608
  772.9 18.3 %slice-start.1 = ((s8[11534336]{0:T(1024)(128)(4,1)}), s8[4194304]{0:T(1024)(128)(4,1)S(1)}, s32[]{:S(2)}) async-start(s8[11534336]{0:T(1024)(128)(4,1)} %bitcast.12), calls=%async_computation.10 | async-start | bytes 8388608
  784.5 7.9 slice-start.2
Sparse Core Ops, SparseCore 0:
  10.3 162.9 reduce-scatter.7
  175.6 158.1 reduce-scatter.5
  336.7 158.0 reduce-scatter.9
  498.3 88.7 all-gather.5
  590.5 89.4 all-gather.3
  683.4 89.4 all-gather.7
where the time goes:
time: 804 us
  waiting for transfers between devices  730 us (91%)
  local copies, waits for them, and re-layouts  51.3 us (6%)
  between operations  14.1 us (2%)
    reduce_scatter x2, waiting for transfers between devices, step(): lax.psum_scatter(t[0], 'dp', scatter_dimension=1, tiled=True)  296 us
    all_gather x3, waiting for transfers between devices, step(): whole = [lax.all_gather(one[0], 'dp', axis=1, tiled=True) for one in new]  274 us
    unnamed x7, waiting for transfers between devices  160 us
    unnamed x22, local copies, waits for them, and re-layouts  51.3 us
  transfers between devices with their start and end apart: 6, of which 6 were waited for; matrix products, arithmetic and copies ran while one was open for 4% of the time, Pallas kernels for 0%

commit v1 on v0

v1 whole, which is shorter than its diff:
```python
import functools

import jax
import jax.numpy as jnp
from jax import lax
from jax.experimental import pallas as pl
from jax.experimental.pallas import tpu as pltpu
from jax.sharding import PartitionSpec as P

MESH = pl.DeviceIdType.MESH
F32, BF16 = jnp.float32, jnp.bfloat16
SPLIT = (128, 128, 96)
HALVES = 2
S1, S2, ZU, ZD, GU, GD, G1, G2, GP = 0, 1, 2, 5, 8, 11, 14, 15, 16
KINDS = 17


def adamw(w, m, v, g):
    m = 0.9 * m + 0.1 * g
    v = 0.95 * v + 0.05 * g * g
    step = m * lax.rsqrt(v + 1e-8) + 0.1 * w
    return (w - 0.02 * step).astype(BF16), m, v


def kernel(split, mats, *refs):
    (g0, g1, g2, w0, w1, w2, m0, m1, m2, v0, v1, v2, out, mo0, mo1, mo2, vo0, vo1, vo2, *scratch) = refs
    own, peer, wb, mb, vb, r1x, r2x, zux, zdx, r1y, r2y, zuy, zdy, r1z, r2z, zuz, zdz, *sems = scratch
    rsem, ssem, lsem, osem, psem, pssem, isem, esem = sems
    units = mats * HALVES
    row = (0, split[0], split[0] + split[1])
    rows = [pl.ds(row[k], split[k]) for k in range(3)]

    me = lax.axis_index("dp")
    c, z, y, x = me % 2, (me // 2) % 4, (me // 8) % 2, me // 16

    def at(x, y, z, c):
        return (0, ((x * 2 + y) * 4 + z) * 2 + c)

    xn, yn, zu, zd, cn = at(1 - x, y, z, c), at(x, 1 - y, z, c), at(x, y, z + 1, c), at(x, y, z - 1, c), at(x, y, z, 1 - c)

    def send(src, dst, k, kind, u, to, land=None):
        pltpu.make_async_remote_copy(
            src_ref=src,
            dst_ref=dst,
            send_sem=ssem.at[k, kind],
            recv_sem=rsem.at[k, kind if land is None else land, u],
            device_id=to,
            device_id_type=MESH,
        ).start()

    def landed(ref, sem):
        pltpu.make_async_copy(ref, ref, sem).wait()

    @pl.when(z == 0)
    def _():
        for ref in (zux, zuy, zuz):
            for u in range(units):
                ref[u] = jnp.zeros(ref.shape[1:], BF16)

    @pl.when(z == 3)
    def _():
        for ref in (zdx, zdy, zdz):
            for u in range(units):
                ref[u] = jnp.zeros(ref.shape[1:], BF16)

    barrier = pltpu.get_barrier_semaphore()
    for to in (xn, yn, cn):
        pl.semaphore_signal(barrier, inc=1, device_id=to, device_id_type=MESH)

    @pl.when(z < 3)
    def _():
        pl.semaphore_signal(barrier, inc=1, device_id=zu, device_id_type=MESH)

    @pl.when(z > 0)
    def _():
        pl.semaphore_signal(barrier, inc=1, device_id=zd, device_id_type=MESH)

    pl.semaphore_wait(barrier, 3 + jnp.where(z > 0, 1, 0) + jnp.where(z < 3, 1, 0))

    for u in range(units):
        mat, h = u // HALVES, u % HALVES
        g = (g0, g1, g2)[mat // 2]
        pltpu.make_async_remote_copy(
            src_ref=g.at[mat % 2, :, :, :, 1 - c, h],
            dst_ref=peer.at[u],
            send_sem=pssem.at[0],
            recv_sem=psem.at[u],
            device_id=cn,
            device_id_type=MESH,
        ).start()
        pltpu.make_async_copy(g.at[mat % 2, :, :, :, c, h], own.at[u], osem.at[u]).start()
    incoming = []
    for a in range(mats // 2):
        two = pl.ds(2 * a, 2)
        incoming.append(pltpu.make_async_copy((w0, w1, w2)[a].at[:, me], wb.at[two], isem.at[a]))
        incoming.append(pltpu.make_async_copy((m0, m1, m2)[a], mb.at[two], isem.at[3 + a]))
        incoming.append(pltpu.make_async_copy((v0, v1, v2)[a], vb.at[two], isem.at[6 + a]))
    for copy in incoming:
        copy.start()

    def total(terms):
        acc = terms[0].astype(F32)
        for term in terms[1:]:
            acc = acc + term.astype(F32)
        return acc

    def loop(n, body):
        lax.fori_loop(0, n, lambda i, _: (body(i), 0)[1], 0)

    def first_colours(k):
        f, s, fn, sn = ((x, y, xn, yn), (y, x, yn, xn))[k]
        r1, r2, up, down = ((r1x, r2x, zux, zdx), (r1y, r2y, zuy, zdy))[k]
        n = rows[k]

        def xy(one, two):
            return (one, two) if k == 0 else (two, one)

        def base(u, zj):
            i = (u, x, y, zj, n)
            return [own[i], peer[i], r1[u, s, zj], r2[u, zj]]

        def a(u):
            def body(i):
                j = (u, *xy(1 - f, i // 4), i % 4, n)
                own[j] = total([own[j], peer[j]]).astype(BF16)

            loop(8, body)
            send(own.at[(u, *xy(1 - f, slice(None)), slice(None), n)], r1.at[u], k, S1, u, fn)

        def b(u):
            landed(r1.at[u], rsem.at[k, S1, u])

            def body(i):
                j = (u, *xy(f, 1 - s), i, n)
                own[j] = total([own[j], peer[j], r1[u, 1 - s, i]]).astype(BF16)

            loop(4, body)
            send(own.at[(u, *xy(f, 1 - s), slice(None), n)], r2.at[u], k, S2, u, sn)

        def hop(u, d):
            if d == 3:
                landed(r2.at[u], rsem.at[k, S2, u])

            @pl.when(z + d <= 3)
            def _():
                if d < 3:
                    pl.when(z > 0)(lambda: landed(up.at[u, d], rsem.at[k, ZU + d, u]))
                i = (u, x, y, z + d, n)
                own[i] = total(base(u, z + d) + ([up[u, d]] if d < 3 else [])).astype(BF16)
                send(own.at[i], up.at[u, d - 1], k, ZU + d - 1, u, zu)

            @pl.when(z - d >= 0)
            def _():
                if d < 3:
                    pl.when(z < 3)(lambda: landed(down.at[u, d], rsem.at[k, ZD + d, u]))
                i = (u, x, y, z - d, n)
                own[i] = total(base(u, z - d) + ([down[u, d]] if d < 3 else [])).astype(BF16)
                send(own.at[i], down.at[u, d - 1], k, ZD + d - 1, u, zd)

        def update(u):
            mat, h = u // HALVES, u % HALVES
            pl.when(z > 0)(lambda: landed(up.at[u, 0], rsem.at[k, ZU, u]))
            pl.when(z < 3)(lambda: landed(down.at[u, 0], rsem.at[k, ZD, u]))

            def body(i):
                p, q = pl.ds(row[k] + i * 16, 16), pl.ds(i * 16, 16)
                j = (u, x, y, z, p)
                g = total([own[j], peer[j], r1[u, s, z, q], r2[u, z, q], up[u, 0, q], down[u, 0, q]]).astype(BF16).astype(F32)
                j = (mat, h, p)
                wb[j], mb[j], vb[j] = adamw(wb[j].astype(F32), mb[j], vb[j], g)

            loop(split[k] // 16, body)
            mine = out.at[mat, x, y, z, c, h, n]
            pltpu.make_async_copy(wb.at[mat, h, n], mine, lsem.at[k, u]).start()
            pl.when(z < 3)(lambda: send(wb.at[mat, h, n], mine, k, GU, u, zu))
            pl.when(z > 0)(lambda: send(wb.at[mat, h, n], mine, k, GD, u, zd))

        def forward(u, d):
            mat, h = u // HALVES, u % HALVES

            @pl.when(z - d >= 0)
            def _():
                ref = out.at[mat, x, y, z - d, c, h, n]
                landed(ref, rsem.at[k, GU + d - 1, u])
                if d < 3:
                    pl.when(z < 3)(lambda: send(ref, ref, k, GU + d, u, zu))

            @pl.when(z + d <= 3)
            def _():
                ref = out.at[mat, x, y, z + d, c, h, n]
                landed(ref, rsem.at[k, GD + d - 1, u])
                if d < 3:
                    pl.when(z > 0)(lambda: send(ref, ref, k, GD + d, u, zd))

        def second(u):
            mat, h = u // HALVES, u % HALVES
            landed(out.at[mat, x, y, z, c, h, n], lsem.at[k, u])
            ref = out.at[mat, x, y, :, c, h, n]
            send(ref, ref, k, G1, u, sn)

        def third(u):
            mat, h = u // HALVES, u % HALVES
            landed(out.at[(mat, *xy(f, 1 - s), slice(None), c, h, n)], rsem.at[k, G1, u])
            ref = out.at[(mat, *xy(f, slice(None)), slice(None), c, h, n)]
            send(ref, ref, k, G2, u, fn)

        def last(u):
            mat, h = u // HALVES, u % HALVES
            landed(out.at[(mat, *xy(1 - f, slice(None)), slice(None), c, h, n)], rsem.at[k, G2, u])
            ref = out.at[mat, :, :, :, c, h, n]
            send(ref, ref, k, GP, u, cn)

        def drain():
            landed(own.at[(slice(None), *xy(1 - f, slice(None)), slice(None), n)], ssem.at[k, S1])
            landed(own.at[(slice(None), *xy(f, 1 - s), slice(None), n)], ssem.at[k, S2])
            for d in (1, 2, 3):
                pl.when(z + d <= 3)(lambda: landed(own.at[:, x, y, z + d, n], ssem.at[k, ZU + d - 1]))
                pl.when(z - d >= 0)(lambda: landed(own.at[:, x, y, z - d, n], ssem.at[k, ZD + d - 1]))
            for d in (0, 1, 2):
                pl.when((z - d >= 0) & (z < 3))(lambda: landed(out.at[:, x, y, z - d, c, :, n], ssem.at[k, GU + d]))
                pl.when((z + d <= 3) & (z > 0))(lambda: landed(out.at[:, x, y, z + d, c, :, n], ssem.at[k, GD + d]))
            landed(out.at[:, x, y, :, c, :, n], ssem.at[k, G1])
            landed(out.at[(slice(None), *xy(f, slice(None)), slice(None), c, slice(None), n)], ssem.at[k, G2])

        return a, b, hop, update, forward, second, third, last, drain

    def z_colour():
        k, n = 2, rows[2]

        def hop(u, d):
            def side(sign, ref, kind, to):
                zj = z + sign * d
                if d < 3:
                    pl.when(z > 0 if sign > 0 else z < 3)(lambda: landed(ref.at[u, d], rsem.at[k, kind + d, u]))

                def body(i):
                    j = (u, i // 2, i % 2, zj, n)
                    own[j] = total([own[j], peer[j]] + ([ref[u, d, i // 2, i % 2]] if d < 3 else [])).astype(BF16)

                loop(4, body)
                send(own.at[u, :, :, zj, n], ref.at[u, d - 1], k, kind + d - 1, u, to)

            pl.when(z + d <= 3)(lambda: side(1, zuz, ZU, zu))
            pl.when(z - d >= 0)(lambda: side(-1, zdz, ZD, zd))

        def base(u, xj, yj):
            i = (u, xj, yj, z, n)
            return [own[i], peer[i], zuz[u, 0, xj, yj], zdz[u, 0, xj, yj]]

        def to_x(u):
            pl.when(z > 0)(lambda: landed(zuz.at[u, 0], rsem.at[k, ZU, u]))
            pl.when(z < 3)(lambda: landed(zdz.at[u, 0], rsem.at[k, ZD, u]))

            def body(i):
                own[u, 1 - x, i, z, n] = total(base(u, 1 - x, i)).astype(BF16)

            loop(2, body)
            send(own.at[u, 1 - x, :, z, n], r1z.at[u], k, S1, u, xn)

        def to_y(u):
            landed(r1z.at[u], rsem.at[k, S1, u])
            i = (u, x, 1 - y, z, n)
            own[i] = total(base(u, x, 1 - y) + [r1z[u, 1 - y]]).astype(BF16)
            send(own.at[i], r2z.at[u], k, S2, u, yn)

        def update(u):
            mat, h = u // HALVES, u % HALVES
            landed(r2z.at[u], rsem.at[k, S2, u])

            def body(i):
                p, q = pl.ds(row[k] + i * 16, 16), pl.ds(i * 16, 16)
                j = (u, x, y, z, p)
                g = total([own[j], peer[j], zuz[u, 0, x, y, q], zdz[u, 0, x, y, q], r1z[u, y, q], r2z[u, q]]).astype(BF16).astype(F32)
                j = (mat, h, p)
                wb[j], mb[j], vb[j] = adamw(wb[j].astype(F32), mb[j], vb[j], g)

            loop(split[k] // 16, body)
            mine = out.at[mat, x, y, z, c, h, n]
            pltpu.make_async_copy(wb.at[mat, h, n], mine, lsem.at[k, u]).start()
            send(wb.at[mat, h, n], mine, k, G1, u, yn)

        def second(u):
            mat, h = u // HALVES, u % HALVES
            landed(out.at[mat, x, y, z, c, h, n], lsem.at[k, u])
            landed(out.at[mat, x, 1 - y, z, c, h, n], rsem.at[k, G1, u])
            ref = out.at[mat, x, :, z, c, h, n]
            send(ref, ref, k, G2, u, xn)

        def third(u):
            mat, h = u // HALVES, u % HALVES
            landed(out.at[mat, 1 - x, :, z, c, h, n], rsem.at[k, G2, u])
            ref = out.at[mat, :, :, z, c, h, n]
            pl.when(z < 3)(lambda: send(ref, ref, k, GU, u, zu))
            pl.when(z > 0)(lambda: send(ref, ref, k, GD, u, zd))

        def forward(u, d):
            mat, h = u // HALVES, u % HALVES

            @pl.when(z - d >= 0)
            def _():
                ref = out.at[mat, :, :, z - d, c, h, n]
                landed(ref, rsem.at[k, GU + d - 1, u])
                if d < 3:
                    pl.when(z < 3)(lambda: send(ref, ref, k, GU + d, u, zu))

            @pl.when(z + d <= 3)
            def _():
                ref = out.at[mat, :, :, z + d, c, h, n]
                landed(ref, rsem.at[k, GD + d - 1, u])
                if d < 3:
                    pl.when(z > 0)(lambda: send(ref, ref, k, GD + d, u, zd))

        def last(u):
            mat, h = u // HALVES, u % HALVES
            ref = out.at[mat, :, :, :, c, h, n]
            send(ref, ref, k, GP, u, cn)

        def drain():
            for d in (1, 2, 3):
                pl.when(z + d <= 3)(lambda: landed(own.at[:, :, :, z + d, n], ssem.at[k, ZU + d - 1]))
                pl.when(z - d >= 0)(lambda: landed(own.at[:, :, :, z - d, n], ssem.at[k, ZD + d - 1]))
            landed(own.at[:, 1 - x, :, z, n], ssem.at[k, S1])
            landed(own.at[:, x, 1 - y, z, n], ssem.at[k, S2])
            landed(out.at[:, x, y, z, c, :, n], ssem.at[k, G1])
            landed(out.at[:, x, :, z, c, :, n], ssem.at[k, G2])
            for d in (0, 1, 2):
                pl.when((z - d >= 0) & (z < 3))(lambda: landed(out.at[:, :, :, z - d, c, :, n], ssem.at[k, GU + d]))
                pl.when((z + d <= 3) & (z > 0))(lambda: landed(out.at[:, :, :, z + d, c, :, n], ssem.at[k, GD + d]))

        return hop, to_x, to_y, update, second, third, forward, last, drain

    xa, xb, xhop, xupdate, xforward, xsecond, xthird, xlast, xdrain = first_colours(0)
    ya, yb, yhop, yupdate, yforward, ysecond, ythird, ylast, ydrain = first_colours(1)
    zhop, zx, zy, zupdate, zsecond, zthird, zforward, zlast, zdrain = z_colour()

    def arrive(u):
        landed(peer.at[u], psem.at[u])
        landed(own.at[u], osem.at[u])

    def moments(u):
        for a in range(mats // 2):

            @pl.when(u == 2 * HALVES * (a + 1) - 1)
            def _():
                two = pl.ds(2 * a, 2)
                pltpu.make_async_copy(mb.at[two], (mo0, mo1, mo2)[a], esem.at[a]).start()
                pltpu.make_async_copy(vb.at[two], (vo0, vo1, vo2)[a], esem.at[3 + a]).start()

    def settle(u):
        for a in range(mats // 2):

            @pl.when(u == 2 * HALVES * a)
            def _():
                for copy in incoming[3 * a : 3 * a + 3]:
                    copy.wait()

    plan = [
        (0, arrive),
        (0, xa),
        (0, ya),
        (0, lambda u: zhop(u, 3)),
        (1, xb),
        (1, yb),
        (0, lambda u: zhop(u, 2)),
        (2, lambda u: xhop(u, 3)),
        (2, lambda u: yhop(u, 3)),
        (2, zx),
        (3, zy),
        (1, lambda u: zhop(u, 1)),
        (2, lambda u: xhop(u, 2)),
        (2, lambda u: yhop(u, 2)),
        (5, zsecond),
        (4, lambda u: xforward(u, 1)),
        (4, lambda u: yforward(u, 1)),
        (6, zthird),
        (5, (lambda u: xforward(u, 3), xsecond)),
        (5, (lambda u: yforward(u, 3), ysecond)),
        (2, lambda u: xhop(u, 1)),
        (2, lambda u: yhop(u, 1)),
        (7, lambda u: zforward(u, 1)),
        (6, xthird),
        (6, ythird),
        (4, lambda u: xforward(u, 2)),
        (4, lambda u: yforward(u, 2)),
        (7, lambda u: zforward(u, 2)),
        (3, settle),
        (3, xupdate),
        (3, yupdate),
        (4, zupdate),
        (4, moments),
        (7, xlast),
        (7, ylast),
        (8, (lambda u: zforward(u, 3), zlast)),
    ]

    def run(stages, u):
        for stage in stages if isinstance(stages, tuple) else (stages,):
            stage(u)

    @pl.loop(0, units + max(lag for lag, _ in plan))
    def _(t):
        for lag, stage in plan:
            u = t - lag
            pl.when((u >= 0) & (u < units))(functools.partial(run, stage, u))

    for k in range(3):

        @pl.loop(0, units)
        def _(u):
            landed(out.at[u // HALVES, :, :, :, 1 - c, u % HALVES, rows[k]], rsem.at[k, GP, u])

        landed(out.at[:, :, :, :, c, :, rows[k]], ssem.at[k, GP])
    for a in range(mats // 2):
        two = pl.ds(2 * a, 2)
        landed(mb.at[two], esem.at[a])
        landed(vb.at[two], esem.at[3 + a])
    landed(peer, pssem.at[0])
    xdrain()
    ydrain()
    zdrain()


def call(terms, weights, m, v, split=SPLIT):
    mats, high = 2 * len(terms), sum(split)
    units = mats * HALVES
    rx, ry, rz = split
    some = jax.ShapeDtypeStruct
    moment = some((2, HALVES, high, 128), F32)
    block = [
        pltpu.VMEM((units, 2, 2, 4, high, 128), BF16),
        pltpu.VMEM((units, 2, 2, 4, high, 128), BF16),
        pltpu.VMEM((mats, HALVES, high, 128), BF16),
        pltpu.VMEM((mats, HALVES, high, 128), F32),
        pltpu.VMEM((mats, HALVES, high, 128), F32),
    ]
    for r in (rx, ry):
        block += [
            pltpu.VMEM((units, 2, 4, r, 128), BF16),
            pltpu.VMEM((units, 4, r, 128), BF16),
            pltpu.VMEM((units, 3, r, 128), BF16),
            pltpu.VMEM((units, 3, r, 128), BF16),
        ]
    block += [
        pltpu.VMEM((units, 2, rz, 128), BF16),
        pltpu.VMEM((units, rz, 128), BF16),
        pltpu.VMEM((units, 3, 2, 2, rz, 128), BF16),
        pltpu.VMEM((units, 3, 2, 2, rz, 128), BF16),
    ]
    dma = pltpu.SemaphoreType.DMA
    return pl.pallas_call(
        functools.partial(kernel, split, mats),
        out_shape=[some((mats, 2, 2, 4, 2, HALVES, high, 128), BF16)] + [moment] * 6,
        in_specs=[pl.BlockSpec(memory_space=pl.ANY)] * 12,
        out_specs=[pl.BlockSpec(memory_space=pl.ANY)] * 7,
        scratch_shapes=block
        + [dma((3, KINDS, units)), dma((3, KINDS)), dma((3, units)), dma((units,)), dma((units,)), dma((1,)), dma((9,)), dma((6,))],
        compiler_params=pltpu.CompilerParams(collective_id=0, has_side_effects=True, vmem_limit_bytes=67043328),
        name="step",
    )(*terms, *weights, *m, *v)


def tiles(a):
    *lead, rows, columns = a.shape
    a = a.reshape(*lead, rows // 8, 8, columns // 128, 128)
    return jnp.swapaxes(a, -3, -2).reshape(*lead, rows * columns // 128, 128)


def untiles(a, rows, columns):
    lead = a.shape[:-2]
    a = a.reshape(*lead, rows // 8, columns // 128, 8, 128)
    return jnp.swapaxes(a, -3, -2).reshape(*lead, rows, columns)


def solution(mesh):
    def step(*arrays):
        terms, weights, m, v = (arrays[i : i + 3] for i in (0, 3, 6, 9))
        high = sum(SPLIT)
        out = call(
            [tiles(t[0]).reshape(2, 2, 2, 4, 2, HALVES, high, 128) for t in terms],
            [tiles(w).reshape(2, 32, HALVES, high, 128) for w in weights],
            [tiles(one).reshape(2, HALVES, high, 128) for one in m],
            [tiles(one).reshape(2, HALVES, high, 128) for one in v],
        )
        whole = [untiles(out[0][2 * i : 2 * i + 2].reshape(2, -1, 128), *w.shape[1:]) for i, w in enumerate(weights)]
        moments = [untiles(one.reshape(2, -1, 128), *old.shape[1:]) for one, old in zip(out[1:], (*m, *v), strict=True)]
        return (*whole, *moments)

    all_of, cut = P(None, None, None), P(None, "dp", None)
    return jax.shard_map(
        step,
        mesh=mesh,
        in_specs=(P(("rep", "dp"), None, None, None),) * 3 + (all_of,) * 3 + (cut,) * 6,
        out_specs=(P("rep", None, None),) * 3 + (P("rep", "dp", None),) * 6,
        check_vma=False,
    )
```

time: 804 us -> 287 us (0.36)
  waiting for transfers between devices: 730 us -> 0 us
  Pallas kernels: 0 us -> 256 us
  local copies, waits for them, and re-layouts: 51.3 us -> 30 us
  between operations: 14.1 us -> 0.71 us
    reduce_scatter x2 -> x0, waiting for transfers between devices: 296 us -> none  [step(): lax.psum_scatter(t[0], 'dp', scatter_dimension=1, tiled=True)]
    all_gather x3 -> x0, waiting for transfers between devices: 274 us -> none  [step(): whole = [lax.all_gather(one[0], 'dp', axis=1, tiled=True) for one in new]]
    pallas_call x0 -> x1, Pallas kernels: none -> 256 us  [call(): pl.pallas_call(functools.partial(kernel, split, mats), out_shape=[some((m...]
    unnamed x7 -> x0, waiting for transfers between devices: 160 us -> none
    unnamed x22 -> x18, local copies, waits for them, and re-layouts: 51.3 us -> 5.17 us
    slice x0 -> x1, local copies, waits for them, and re-layouts: none -> 24.8 us  [step(): out[0][2 * i:2 * i + 2].reshape(2, -1, 128)]
  transfers between devices with their start and end apart: 6 -> 0, of which waited for: 6 -> 0; matrix products, arithmetic and copies ran while one was open for 4% -> 0% of each run, Pallas kernels for 0% -> 0%
where the time goes in v1:
time: 287 us
  Pallas kernels  256 us (89%)
  local copies, waits for them, and re-layouts  30 us (10%)
    pallas_call x1, Pallas kernels, call(): pl.pallas_call(functools.partial(kernel, split, mats), out_shape=[some((m...  256 us
    slice x1, local copies, waits for them, and re-layouts, step(): out[0][2 * i:2 * i + 2].reshape(2, -1, 128)  24.8 us

profile of v1, /device:TPU:0, one launch (start us, length us, event | category | flops | bytes accessed | tf_op | source)
XLA Modules:
  0.0 286.5 jit_solution(11292761727546725861)
XLA Ops:
  0.6 255.8 %step.1 = (bf16[6,2,2,4,2,2,352,128]{7,6,5,4,3,2,1,0:T(8,128)(2,1)}, f32[2,2,352,128]{3,2,1,0:T(8,128)}, f32[2,2,352,128]{3,2,1,0:T(8,128)}, f32[2,2,352,128]{3,...) custom-call(bf16[2,2,2,4,2,2,352,128]{7,6,5,4,3,2,1,0:T(8,128)(2,1)} %bitcast.105, ...), custom_call_target="tpu_custom_call" | custom-call | tf_op jit(solution)/shard_map/step/pallas_call | solution.py:450
  256.5 0.0 copy-start.5
  256.5 0.0 copy-start.4
  256.5 0.0 copy-start.3
  256.5 0.0 copy-start.2
  256.5 0.0 copy-start.1
  256.5 0.0 copy-start
  256.5 24.8 %fusion = (bf16[2,2,2,4,2,2,352,128]{7,6,5,4,3,2,1,0:T(8,128)(2,1)}, bf16[2,2,2,4,2,2,352,128]{7,6,5,4,3,2,1,0:T(8,128)(2,1)}, bf16[2,2,2,4,2,2,352,128]{7,6,5,4,3,2,1,0:T(8,128)(2,1)}) fusion(bf16[6,2,2,4,2,2,352,128]{7,6,5,4,3,2,1,0:T(8,128)(2,1)} %get-tuple-element.16), kind=kLoop, calls=%fused_computation | loop fusion | bytes 69206016 | tf_op jit(solution)/shard_map/slice | solution.py:484
  281.4 0.0 copy-done.5
  281.4 0.9 copy.27
  282.2 0.0 copy-done.4
  282.2 0.9 copy.28
  283.1 0.0 copy-done.3
  283.1 0.9 copy.29
  283.9 0.0 copy-done.2
  283.9 0.9 copy.30
  284.8 0.0 copy-done.1
  284.8 0.9 copy.31
  285.7 0.0 copy-done
  285.7 0.9 copy.32
Async XLA Ops:
  256.5 24.9 %copy-start.5 = (f32[2,2,352,128]{3,2,1,0:T(8,128)S(1)}, f32[2,2,352,128]{3,2,1,0:T(8,128)}, u32[]{:S(2)}) copy-start(f32[2,2,352,128]{3,2,1,0:T(8,128)} %get-tuple-element.17) | copy-start | bytes 2162692
  256.5 25.7 %copy-start.4 = (f32[2,2,352,128]{3,2,1,0:T(8,128)S(1)}, f32[2,2,352,128]{3,2,1,0:T(8,128)}, u32[]{:S(2)}) copy-start(f32[2,2,352,128]{3,2,1,0:T(8,128)} %get-tuple-element.18) | copy-start | bytes 2162692
  256.5 26.6 %copy-start.3 = (f32[2,2,352,128]{3,2,1,0:T(8,128)S(1)}, f32[2,2,352,128]{3,2,1,0:T(8,128)}, u32[]{:S(2)}) copy-start(f32[2,2,352,128]{3,2,1,0:T(8,128)} %get-tuple-element.19) | copy-start | bytes 2162692
  256.5 27.4 %copy-start.2 = (f32[2,2,352,128]{3,2,1,0:T(8,128)S(1)}, f32[2,2,352,128]{3,2,1,0:T(8,128)}, u32[]{:S(2)}) copy-start(f32[2,2,352,128]{3,2,1,0:T(8,128)} %get-tuple-element.20) | copy-start | bytes 2162692
  256.5 28.3 %copy-start.1 = (f32[2,2,352,128]{3,2,1,0:T(8,128)S(1)}, f32[2,2,352,128]{3,2,1,0:T(8,128)}, u32[]{:S(2)}) copy-start(f32[2,2,352,128]{3,2,1,0:T(8,128)} %get-tuple-element.21) | copy-start | bytes 2162692
  256.5 29.1 %copy-start = (f32[2,2,352,128]{3,2,1,0:T(8,128)S(1)}, f32[2,2,352,128]{3,2,1,0:T(8,128)}, u32[]{:S(2)}) copy-start(f32[2,2,352,128]{3,2,1,0:T(8,128)} %get-tuple-element.22) | copy-start | bytes 2162692

commit v2 on v1

v2 whole, which is shorter than its diff:
```python
import functools
import math

import jax
import jax.numpy as jnp
from jax import lax
from jax.experimental import pallas as pl
from jax.experimental.pallas import tpu as pltpu
from jax.sharding import PartitionSpec as P

MESH = pl.DeviceIdType.MESH
F32, BF16 = jnp.float32, jnp.bfloat16
SPLIT = (128, 128, 96)
HALVES = 2
PLAN = (
    (0, "arrive", 0),
    (9, "f2", 2),
    (5, "free", 2),
    (1, "b", 1),
    (4, "free", 1),
    (0, "a", 1),
    (4, "go", 0),
    (4, "go", 1),
    (10, "f3", 2),
    (0, "a", 0),
    (3, "h1", 1),
    (6, "s", 2),
    (7, "t", 2),
    (0, "h3", 2),
    (8, "t", 0),
    (3, "b", 2),
    (8, "l", 1),
    (3, "h1", 0),
    (5, "f3", 0),
    (2, "h3", 0),
    (5, "f3", 1),
    (4, "f1", 0),
    (5, "go", 2),
    (4, "f1", 1),
    (1, "b", 0),
    (10, "l", 2),
    (5, "s", 1),
    (1, "h1", 2),
    (6, "s", 0),
    (6, "t", 1),
    (4, "f2", 0),
    (7, "f1", 2),
    (4, "up", 2),
    (2, "a", 2),
    (0, "h2", 2),
    (3, "up", 0),
    (3, "free", 0),
    (3, "up", 1),
    (1, "h3", 1),
    (4, "f2", 1),
    (2, "h2", 1),
    (11, "l", 0),
    (2, "h2", 0),
)
S1, S2, ZU, ZD, GU, GD, G1, G2, GP = 0, 1, 2, 5, 8, 11, 14, 15, 16
SCATTER, KINDS = 8, 17
X, Y, UP, DOWN, CORE = range(5)


def adamw(w, m, v, g):
    m = 0.9 * m + 0.1 * g
    v = 0.95 * v + 0.05 * g * g
    step = m * lax.rsqrt(v + 1e-8) + 0.1 * w
    return (w - 0.02 * step).astype(BF16), m, v


def kernel(split, mats, *refs):
    (g0, g1, g2, w0, w1, w2, m0, m1, m2, v0, v1, v2, own, peer, mb, vb, *scratch) = refs
    wb, r1x, r2x, zux, zdx, r1y, r2y, zuy, zdy, r1z, r2z, zuz, zdz, *sems = scratch
    rsem, ssem, gsem, osem, psem, pssem, isem, credit = sems
    units = mats * HALVES
    row = (0, split[0], split[0] + split[1])
    rows = [pl.ds(row[k], split[k]) for k in range(3)]

    me = lax.axis_index("dp")
    c, z, y, x = me % 2, (me // 2) % 4, (me // 8) % 2, me // 16

    def at(x, y, z, c):
        return (0, ((x * 2 + y) * 4 + z) * 2 + c)

    xn, yn, zu, zd, cn = at(1 - x, y, z, c), at(x, 1 - y, z, c), at(x, y, z + 1, c), at(x, y, z - 1, c), at(x, y, z, 1 - c)

    def send(src, dst, k, kind, u, to, land=None):
        pltpu.make_async_remote_copy(
            src_ref=src,
            dst_ref=dst,
            send_sem=ssem.at[k, kind, u] if kind < SCATTER else gsem.at[k, kind - SCATTER],
            recv_sem=rsem.at[k, kind if land is None else land, u],
            device_id=to,
            device_id_type=MESH,
        ).start()

    def landed(ref, sem):
        pltpu.make_async_copy(ref, ref, sem).wait()

    def give(k):
        for side, to in ((X, xn), (Y, yn), (CORE, cn)):
            pl.semaphore_signal(credit.at[k, side], inc=1, device_id=to, device_id_type=MESH)
        pl.when(z < 3)(lambda: pl.semaphore_signal(credit.at[k, DOWN], inc=1, device_id=zu, device_id_type=MESH))
        pl.when(z > 0)(lambda: pl.semaphore_signal(credit.at[k, UP], inc=1, device_id=zd, device_id_type=MESH))

    def take(k, side):
        pl.semaphore_wait(credit.at[k, side], 1)

    @pl.when(z == 0)
    def _():
        for ref in (zux, zuy, zuz):
            for u in range(units):
                ref[u] = jnp.zeros(ref.shape[1:], BF16)

    @pl.when(z == 3)
    def _():
        for ref in (zdx, zdy, zdz):
            for u in range(units):
                ref[u] = jnp.zeros(ref.shape[1:], BF16)

    barrier = pltpu.get_barrier_semaphore()
    for to in (xn, yn, cn):
        pl.semaphore_signal(barrier, inc=1, device_id=to, device_id_type=MESH)

    @pl.when(z < 3)
    def _():
        pl.semaphore_signal(barrier, inc=1, device_id=zu, device_id_type=MESH)

    @pl.when(z > 0)
    def _():
        pl.semaphore_signal(barrier, inc=1, device_id=zd, device_id_type=MESH)

    pl.semaphore_wait(barrier, 3 + jnp.where(z > 0, 1, 0) + jnp.where(z < 3, 1, 0))

    for u in range(units):
        mat, h = u // HALVES, u % HALVES
        g = (g0, g1, g2)[mat // 2]
        pltpu.make_async_remote_copy(
            src_ref=g.at[mat % 2, :, :, :, 1 - c, h],
            dst_ref=peer.at[u],
            send_sem=pssem.at[0],
            recv_sem=psem.at[u],
            device_id=cn,
            device_id_type=MESH,
        ).start()
        pltpu.make_async_copy(g.at[mat % 2, :, :, :, c, h], own.at[u], osem.at[u]).start()
    incoming = []
    for a in range(mats // 2):
        two = pl.ds(2 * a, 2)
        incoming.append(pltpu.make_async_copy((w0, w1, w2)[a].at[:, me], wb.at[two], isem.at[a]))
        incoming.append(pltpu.make_async_copy((m0, m1, m2)[a], mb.at[two], isem.at[3 + a]))
        incoming.append(pltpu.make_async_copy((v0, v1, v2)[a], vb.at[two], isem.at[6 + a]))
    for copy in incoming:
        copy.start()

    def total(terms):
        acc = terms[0].astype(F32)
        for term in terms[1:]:
            acc = acc + term.astype(F32)
        return acc

    def loop(n, body):
        lax.fori_loop(0, n, lambda i, _: (body(i), 0)[1], 0)

    def hops(hop, forward):
        scatter = {f"h{d}": functools.partial(hop, d=d) for d in (1, 2, 3)}
        return scatter | {f"f{d}": functools.partial(forward, d=d) for d in (1, 2, 3)}

    def first_colours(k):
        f, s, fn, sn = ((x, y, xn, yn), (y, x, yn, xn))[k]
        first_side, second_side = ((X, Y), (Y, X))[k]
        r1, r2, up, down = ((r1x, r2x, zux, zdx), (r1y, r2y, zuy, zdy))[k]
        n = rows[k]

        def xy(one, two):
            return (one, two) if k == 0 else (two, one)

        def base(u, zj):
            i = (u, x, y, zj, n)
            return [own[i], peer[i], r1[u, s, zj], r2[u, zj]]

        def a(u):
            def body(i):
                j = (u, *xy(1 - f, i // 4), i % 4, n)
                own[j] = total([own[j], peer[j]]).astype(BF16)

            loop(8, body)
            send(own.at[(u, *xy(1 - f, slice(None)), slice(None), n)], r1.at[u], k, S1, u, fn)

        def b(u):
            landed(r1.at[u], rsem.at[k, S1, u])

            def body(i):
                j = (u, *xy(f, 1 - s), i, n)
                own[j] = total([own[j], peer[j], r1[u, 1 - s, i]]).astype(BF16)

            loop(4, body)
            send(own.at[(u, *xy(f, 1 - s), slice(None), n)], r2.at[u], k, S2, u, sn)

        def hop(u, d):
            if d == 3:
                landed(r2.at[u], rsem.at[k, S2, u])

            @pl.when(z + d <= 3)
            def _():
                if d < 3:
                    pl.when(z > 0)(lambda: landed(up.at[u, d], rsem.at[k, ZU + d, u]))
                i = (u, x, y, z + d, n)
                own[i] = total(base(u, z + d) + ([up[u, d]] if d < 3 else [])).astype(BF16)
                send(own.at[i], up.at[u, d - 1], k, ZU + d - 1, u, zu)

            @pl.when(z - d >= 0)
            def _():
                if d < 3:
                    pl.when(z < 3)(lambda: landed(down.at[u, d], rsem.at[k, ZD + d, u]))
                i = (u, x, y, z - d, n)
                own[i] = total(base(u, z - d) + ([down[u, d]] if d < 3 else [])).astype(BF16)
                send(own.at[i], down.at[u, d - 1], k, ZD + d - 1, u, zd)

        def update(u):
            mat, h = u // HALVES, u % HALVES
            pl.when(z > 0)(lambda: landed(up.at[u, 0], rsem.at[k, ZU, u]))
            pl.when(z < 3)(lambda: landed(down.at[u, 0], rsem.at[k, ZD, u]))

            def body(i):
                p, q = pl.ds(row[k] + i * 16, 16), pl.ds(i * 16, 16)
                j = (u, x, y, z, p)
                g = total([own[j], peer[j], r1[u, s, z, q], r2[u, z, q], up[u, 0, q], down[u, 0, q]]).astype(BF16).astype(F32)
                i = (mat, h, p)
                own[j], mb[i], vb[i] = adamw(wb[i].astype(F32), mb[i], vb[i], g)

            loop(split[k] // 16, body)

        def free(u):
            landed(own.at[(u, *xy(1 - f, slice(None)), slice(None), n)], ssem.at[k, S1, u])
            landed(own.at[(u, *xy(f, 1 - s), slice(None), n)], ssem.at[k, S2, u])
            for d in (1, 2, 3):
                pl.when(z + d <= 3)(lambda: landed(own.at[u, x, y, z + d, n], ssem.at[k, ZU + d - 1, u]))
                pl.when(z - d >= 0)(lambda: landed(own.at[u, x, y, z - d, n], ssem.at[k, ZD + d - 1, u]))
            give(k)

        def go(u):
            mine = own.at[u, x, y, z, n]

            @pl.when(z < 3)
            def _():
                take(k, UP)
                send(mine, mine, k, GU, u, zu)

            @pl.when(z > 0)
            def _():
                take(k, DOWN)
                send(mine, mine, k, GD, u, zd)

        def forward(u, d):

            @pl.when(z - d >= 0)
            def _():
                ref = own.at[u, x, y, z - d, n]
                landed(ref, rsem.at[k, GU + d - 1, u])
                if d < 3:
                    pl.when(z < 3)(lambda: send(ref, ref, k, GU + d, u, zu))

            @pl.when(z + d <= 3)
            def _():
                ref = own.at[u, x, y, z + d, n]
                landed(ref, rsem.at[k, GD + d - 1, u])
                if d < 3:
                    pl.when(z > 0)(lambda: send(ref, ref, k, GD + d, u, zd))

        def second(u):
            ref = own.at[u, x, y, :, n]
            take(k, second_side)
            send(ref, ref, k, G1, u, sn)

        def third(u):
            landed(own.at[(u, *xy(f, 1 - s), slice(None), n)], rsem.at[k, G1, u])
            ref = own.at[(u, *xy(f, slice(None)), slice(None), n)]
            take(k, first_side)
            send(ref, ref, k, G2, u, fn)

        def last(u):
            landed(own.at[(u, *xy(1 - f, slice(None)), slice(None), n)], rsem.at[k, G2, u])
            ref = own.at[u, :, :, :, n]
            take(k, CORE)
            send(ref, peer.at[u, :, :, :, n], k, GP, u, cn)

        def drain():
            for d in (0, 1, 2):
                pl.when((z - d >= 0) & (z < 3))(lambda: landed(own.at[:, x, y, z - d, n], gsem.at[k, GU + d - SCATTER]))
                pl.when((z + d <= 3) & (z > 0))(lambda: landed(own.at[:, x, y, z + d, n], gsem.at[k, GD + d - SCATTER]))
            landed(own.at[:, x, y, :, n], gsem.at[k, G1 - SCATTER])
            landed(own.at[(slice(None), *xy(f, slice(None)), slice(None), n)], gsem.at[k, G2 - SCATTER])

        return dict(a=a, b=b, **hops(hop, forward), up=update, free=free, go=go, s=second, t=third, l=last), drain

    def z_colour():
        k, n = 2, rows[2]

        def hop(u, d):
            def side(sign, ref, kind, to):
                zj = z + sign * d
                if d < 3:
                    pl.when(z > 0 if sign > 0 else z < 3)(lambda: landed(ref.at[u, d], rsem.at[k, kind + d, u]))

                def body(i):
                    j = (u, i // 2, i % 2, zj, n)
                    own[j] = total([own[j], peer[j]] + ([ref[u, d, i // 2, i % 2]] if d < 3 else [])).astype(BF16)

                loop(4, body)
                send(own.at[u, :, :, zj, n], ref.at[u, d - 1], k, kind + d - 1, u, to)

            pl.when(z + d <= 3)(lambda: side(1, zuz, ZU, zu))
            pl.when(z - d >= 0)(lambda: side(-1, zdz, ZD, zd))

        def base(u, xj, yj):
            i = (u, xj, yj, z, n)
            return [own[i], peer[i], zuz[u, 0, xj, yj], zdz[u, 0, xj, yj]]

        def to_x(u):
            pl.when(z > 0)(lambda: landed(zuz.at[u, 0], rsem.at[k, ZU, u]))
            pl.when(z < 3)(lambda: landed(zdz.at[u, 0], rsem.at[k, ZD, u]))

            def body(i):
                own[u, 1 - x, i, z, n] = total(base(u, 1 - x, i)).astype(BF16)

            loop(2, body)
            send(own.at[u, 1 - x, :, z, n], r1z.at[u], k, S1, u, xn)

        def to_y(u):
            landed(r1z.at[u], rsem.at[k, S1, u])
            i = (u, x, 1 - y, z, n)
            own[i] = total(base(u, x, 1 - y) + [r1z[u, 1 - y]]).astype(BF16)
            send(own.at[i], r2z.at[u], k, S2, u, yn)

        def update(u):
            mat, h = u // HALVES, u % HALVES
            landed(r2z.at[u], rsem.at[k, S2, u])

            def body(i):
                p, q = pl.ds(row[k] + i * 16, 16), pl.ds(i * 16, 16)
                j = (u, x, y, z, p)
                g = total([own[j], peer[j], zuz[u, 0, x, y, q], zdz[u, 0, x, y, q], r1z[u, y, q], r2z[u, q]]).astype(BF16).astype(F32)
                i = (mat, h, p)
                own[j], mb[i], vb[i] = adamw(wb[i].astype(F32), mb[i], vb[i], g)

            loop(split[k] // 16, body)

        def free(u):
            for d in (1, 2, 3):
                pl.when(z + d <= 3)(lambda: landed(own.at[u, :, :, z + d, n], ssem.at[k, ZU + d - 1, u]))
                pl.when(z - d >= 0)(lambda: landed(own.at[u, :, :, z - d, n], ssem.at[k, ZD + d - 1, u]))
            landed(own.at[u, 1 - x, :, z, n], ssem.at[k, S1, u])
            landed(own.at[u, x, 1 - y, z, n], ssem.at[k, S2, u])
            give(k)

        def go(u):
            mine = own.at[u, x, y, z, n]
            take(k, Y)
            send(mine, mine, k, G1, u, yn)

        def second(u):
            landed(own.at[u, x, 1 - y, z, n], rsem.at[k, G1, u])
            ref = own.at[u, x, :, z, n]
            take(k, X)
            send(ref, ref, k, G2, u, xn)

        def third(u):
            landed(own.at[u, 1 - x, :, z, n], rsem.at[k, G2, u])
            ref = own.at[u, :, :, z, n]

            @pl.when(z < 3)
            def _():
                take(k, UP)
                send(ref, ref, k, GU, u, zu)

            @pl.when(z > 0)
            def _():
                take(k, DOWN)
                send(ref, ref, k, GD, u, zd)

        def forward(u, d):

            @pl.when(z - d >= 0)
            def _():
                ref = own.at[u, :, :, z - d, n]
                landed(ref, rsem.at[k, GU + d - 1, u])
                if d < 3:
                    pl.when(z < 3)(lambda: send(ref, ref, k, GU + d, u, zu))

            @pl.when(z + d <= 3)
            def _():
                ref = own.at[u, :, :, z + d, n]
                landed(ref, rsem.at[k, GD + d - 1, u])
                if d < 3:
                    pl.when(z > 0)(lambda: send(ref, ref, k, GD + d, u, zd))

        def last(u):
            ref = own.at[u, :, :, :, n]
            take(k, CORE)
            send(ref, peer.at[u, :, :, :, n], k, GP, u, cn)

        def drain():
            landed(own.at[:, x, y, z, n], gsem.at[k, G1 - SCATTER])
            landed(own.at[:, x, :, z, n], gsem.at[k, G2 - SCATTER])
            for d in (0, 1, 2):
                pl.when((z - d >= 0) & (z < 3))(lambda: landed(own.at[:, :, :, z - d, n], gsem.at[k, GU + d - SCATTER]))
                pl.when((z + d <= 3) & (z > 0))(lambda: landed(own.at[:, :, :, z + d, n], gsem.at[k, GD + d - SCATTER]))

        return dict(a=to_x, b=to_y, **hops(hop, forward), up=update, free=free, go=go, s=second, t=third, l=last), drain

    def arrive(u):
        landed(peer.at[u], psem.at[u])
        landed(own.at[u], osem.at[u])

        @pl.when(u == 1)
        def _():
            for copy in incoming:
                copy.wait()

    colours = [first_colours(0), first_colours(1), z_colour()]
    plan = [(lag, arrive if name == "arrive" else colours[k][0][name]) for lag, name, k in PLAN]

    @pl.loop(0, units + max(lag for lag, _ in plan))
    def _(t):
        for lag, stage in plan:
            u = t - lag
            pl.when((u >= 0) & (u < units))(functools.partial(stage, u))

    for k in range(3):

        @pl.loop(0, units)
        def _(u):
            landed(peer.at[u, :, :, :, rows[k]], rsem.at[k, GP, u])

        landed(own.at[:, :, :, :, rows[k]], gsem.at[k, GP - SCATTER])
        colours[k][1]()
    landed(peer, pssem.at[0])


def flush(*refs):
    own, peer, mb, vb, *whole = refs[:7]
    moments, sem = refs[7:13], refs[13]
    c = lax.axis_index("dp") % 2
    copies = []
    for u in range(own.shape[0]):
        mat, h = u // HALVES, u % HALVES
        copies.append((own.at[u], whole[mat // 2].at[mat % 2, :, :, :, c, h]))
        copies.append((peer.at[u], whole[mat // 2].at[mat % 2, :, :, :, 1 - c, h]))
    for a in range(3):
        copies.append((mb.at[pl.ds(2 * a, 2)], moments[a]))
        copies.append((vb.at[pl.ds(2 * a, 2)], moments[3 + a]))
    copies = [pltpu.make_async_copy(src, dst, sem.at[i]) for i, (src, dst) in enumerate(copies)]
    for copy in copies:
        copy.start()
    for copy in copies:
        copy.wait()


def call(terms, weights, m, v, split=SPLIT):
    mats, high = 2 * len(terms), sum(split)
    units = mats * HALVES
    rx, ry, rz = split
    block = [((mats, HALVES, high, 128), BF16)]
    for r in (rx, ry):
        block += [((units, 2, 4, r, 128), BF16), ((units, 4, r, 128), BF16)] + [((units, 3, r, 128), BF16)] * 2
    block += [((units, 2, rz, 128), BF16), ((units, rz, 128), BF16)] + [((units, 3, 2, 2, rz, 128), BF16)] * 2
    scratch = sum(math.prod(shape) * 2 for shape, _ in block)
    dma = pltpu.SemaphoreType.DMA
    half, moment = (units, 2, 2, 4, high, 128), (mats, HALVES, high, 128)
    held = pl.pallas_call(
        functools.partial(kernel, split, mats),
        out_shape=[pltpu.VMEM(half, BF16)] * 2 + [pltpu.VMEM(moment, F32)] * 2,
        in_specs=[pl.BlockSpec(memory_space=pltpu.HBM)] * 12,
        out_specs=[pl.BlockSpec(memory_space=pltpu.VMEM)] * 4,
        scratch_shapes=[pltpu.VMEM(*one) for one in block]
        + [dma((3, KINDS, units)), dma((3, SCATTER, units)), dma((3, KINDS - SCATTER)), dma((units,)), dma((units,)), dma((1,)), dma((9,))]
        + [pltpu.SemaphoreType.REGULAR((3, 5))],
        compiler_params=pltpu.CompilerParams(collective_id=0, has_side_effects=True, vmem_limit_bytes=scratch + (1 << 16)),
        name="step",
    )(*[pltpu.with_memory_space_constraint(one, pltpu.HBM) for one in (*terms, *weights, *m, *v)])
    some = jax.ShapeDtypeStruct
    return pl.pallas_call(
        flush,
        out_shape=[some((2, 2, 2, 4, 2, HALVES, high, 128), BF16)] * 3 + [some((2, HALVES, high, 128), F32)] * 6,
        in_specs=[pl.BlockSpec(memory_space=pltpu.VMEM)] * 4,
        out_specs=[pl.BlockSpec(memory_space=pltpu.HBM)] * 9,
        scratch_shapes=[dma((2 * units + 6,))],
        compiler_params=pltpu.CompilerParams(has_side_effects=True, vmem_limit_bytes=scratch + (1 << 16)),
        name="flush",
    )(*[pltpu.with_memory_space_constraint(one, pltpu.VMEM) for one in held])


def tiles(a):
    *lead, rows, columns = a.shape
    a = a.reshape(*lead, rows // 8, 8, columns // 128, 128)
    return jnp.swapaxes(a, -3, -2).reshape(*lead, rows * columns // 128, 128)


def untiles(a, rows, columns):
    lead = a.shape[:-2]
    a = a.reshape(*lead, rows // 8, columns // 128, 8, 128)
    return jnp.swapaxes(a, -3, -2).reshape(*lead, rows, columns)


def solution(mesh):
    def step(*arrays):
        terms, weights, m, v = (arrays[i : i + 3] for i in (0, 3, 6, 9))
        high = sum(SPLIT)
        out = call(
            [tiles(t[0]).reshape(2, 2, 2, 4, 2, HALVES, high, 128) for t in terms],
            [tiles(w).reshape(2, 32, HALVES, high, 128) for w in weights],
            [tiles(one).reshape(2, HALVES, high, 128) for one in m],
            [tiles(one).reshape(2, HALVES, high, 128) for one in v],
        )
        whole = [untiles(one.reshape(2, -1, 128), *w.shape[1:]) for one, w in zip(out, weights)]
        moments = [untiles(one.reshape(2, -1, 128), *old.shape[1:]) for one, old in zip(out[3:], (*m, *v), strict=True)]
        return (*whole, *moments)

    all_of, cut = P(None, None, None), P(None, "dp", None)
    return jax.shard_map(
        step,
        mesh=mesh,
        in_specs=(P(("rep", "dp"), None, None, None),) * 3 + (all_of,) * 3 + (cut,) * 6,
        out_specs=(P("rep", None, None),) * 3 + (P("rep", "dp", None),) * 6,
        check_vma=False,
    )
```

time: 287 us -> 263 us (0.916)
  local copies, waits for them, and re-layouts: 30 us -> 0 us
  Pallas kernels: 256 us -> 262 us
    slice x1 -> x0, local copies, waits for them, and re-layouts: 24.8 us -> none  [step(): out[0][2 * i:2 * i + 2].reshape(2, -1, 128)]
    pallas_call x1 -> x2, Pallas kernels: 256 us -> 262 us  [the longest x1 249 us: call(): pl.pallas_call(functools.partial(kernel, split, mats), out_shape=[pltpu.V...]
    unnamed x18 -> x0, local copies, waits for them, and re-layouts: 5.17 us -> none
where the time goes in v2:
time: 263 us
  Pallas kernels  262 us (100%)
    pallas_call x1, Pallas kernels, call(): pl.pallas_call(functools.partial(kernel, split, mats), out_shape=[pltpu.V...  249 us
    pallas_call x1, Pallas kernels, call(): pl.pallas_call(flush, out_shape=[some((2, 2, 2, 4, 2, HALVES, high, 128),...  12.7 us

profile of v2, /device:TPU:0, one launch (start us, length us, event | category | flops | bytes accessed | tf_op | source)
XLA Modules:
  0.0 262.5 jit_solution(9803850453652352247)
XLA Ops:
  0.6 249.1 %step.1 = (bf16[12,2,2,4,352,128]{5,4,3,2,1,0:T(8,128)(2,1)S(1)}, bf16[12,2,2,4,352,128]{5,4,3,2,1,0:T(8,128)(2,1)S(1)}, f32[6,2,352,128]{3,2,1,0:T(8,128)S(1)}, f32[6,2,352,128]{3,2,1,0:T(8,128)S(1)}) custom-call(bf16[2,2,2,4,2,2,352,128]{7,6,5,4,3,2,1,0:T(8,128)(2,1)} %bitcast.105, bf16[2,2,2,4,2,2,352,128]{7,6,5,4,3,2,1,0:T(8,128)(2,1)} %bitcast.106, ...), custom_call_target="tpu_custom_call" | custom-call | tf_op jit(solution)/shard_map/step/pallas_call | solution.py:472
  249.8 12.7 %flush.1 = (bf16[2,2,2,4,2,2,352,128]{7,6,5,4,3,2,1,0:T(8,128)(2,1)}, bf16[2,2,2,4,2,2,352,128]{7,6,5,4,3,2,1,0:T(8,128)(2,1)}, bf16[2,2,2,4,2,2,352,128]{7,6,5,...) custom-call(bf16[12,2,2,4,352,128]{5,4,3,2,1,0:T(8,128)(2,1)S(1)} %g, ...), custom_call_target="tpu_custom_call" | custom-call | tf_op jit(solution)/shard_map/flush/pallas_call | solution.py:484

commit v3 on v2

--- a/solution.py
+++ b/solution.py
@@ -10,52 +10,52 @@
 
 MESH = pl.DeviceIdType.MESH
 F32, BF16 = jnp.float32, jnp.bfloat16
-SPLIT = (128, 128, 96)
+SPLIT = (112, 128, 112)
 HALVES = 2
 PLAN = (
     (0, "arrive", 0),
-    (9, "f2", 2),
-    (5, "free", 2),
-    (1, "b", 1),
-    (4, "free", 1),
+    (5, "go", 2),
+    (6, "f1", 0),
+    (2, "b", 1),
+    (2, "b", 0),
+    (7, "s", 1),
+    (8, "t", 0),
+    (7, "t", 2),
+    (4, "h2", 0),
+    (4, "h2", 1),
+    (1, "h2", 2),
+    (5, "up", 0),
+    (5, "free", 0),
+    (3, "h3", 0),
+    (10, "l", 2),
+    (8, "t", 1),
+    (6, "f2", 0),
+    (6, "f2", 1),
+    (5, "up", 1),
+    (5, "go", 0),
+    (5, "free", 1),
+    (5, "go", 1),
+    (0, "h3", 2),
+    (3, "h3", 1),
+    (10, "l", 1),
     (0, "a", 1),
-    (4, "go", 0),
-    (4, "go", 1),
-    (10, "f3", 2),
+    (9, "l", 0),
+    (8, "f2", 2),
+    (6, "f3", 0),
     (0, "a", 0),
-    (3, "h1", 1),
-    (6, "s", 2),
-    (7, "t", 2),
-    (0, "h3", 2),
-    (8, "t", 0),
+    (7, "f1", 2),
+    (6, "s", 0),
+    (4, "h1", 0),
+    (4, "h1", 1),
+    (4, "up", 2),
+    (4, "free", 2),
+    (9, "f3", 2),
+    (1, "h1", 2),
+    (5, "s", 2),
     (3, "b", 2),
-    (8, "l", 1),
-    (3, "h1", 0),
-    (5, "f3", 0),
-    (2, "h3", 0),
-    (5, "f3", 1),
-    (4, "f1", 0),
-    (5, "go", 2),
-    (4, "f1", 1),
-    (1, "b", 0),
-    (10, "l", 2),
-    (5, "s", 1),
-    (1, "h1", 2),
-    (6, "s", 0),
-    (6, "t", 1),
-    (4, "f2", 0),
-    (7, "f1", 2),
-    (4, "up", 2),
+    (6, "f3", 1),
     (2, "a", 2),
-    (0, "h2", 2),
-    (3, "up", 0),
-    (3, "free", 0),
-    (3, "up", 1),
-    (1, "h3", 1),
-    (4, "f2", 1),
-    (2, "h2", 1),
-    (11, "l", 0),
-    (2, "h2", 0),
+    (5, "f1", 1),
 )
 S1, S2, ZU, ZD, GU, GD, G1, G2, GP = 0, 1, 2, 5, 8, 11, 14, 15, 16
 SCATTER, KINDS = 8, 17
@@ -106,18 +106,6 @@
 
     def take(k, side):
         pl.semaphore_wait(credit.at[k, side], 1)
-
-    @pl.when(z == 0)
-    def _():
-        for ref in (zux, zuy, zuz):
-            for u in range(units):
-                ref[u] = jnp.zeros(ref.shape[1:], BF16)
-
-    @pl.when(z == 3)
-    def _():
-        for ref in (zdx, zdy, zdz):
-            for u in range(units):
-                ref[u] = jnp.zeros(ref.shape[1:], BF16)
 
     barrier = pltpu.get_barrier_semaphore()
     for to in (xn, yn, cn):
@@ -153,6 +141,21 @@
         incoming.append(pltpu.make_async_copy((v0, v1, v2)[a], vb.at[two], isem.at[6 + a]))
     for copy in incoming:
         copy.start()
+
+    def blank(ref):
+        @pl.loop(0, units)
+        def _(u):
+            ref[u] = jnp.zeros(ref.shape[1:], BF16)
+
+    @pl.when(z == 0)
+    def _():
+        for ref in (zux, zuy, zuz):
+            blank(ref)
+
+    @pl.when(z == 3)
+    def _():
+        for ref in (zdx, zdy, zdz):
+            blank(ref)
 
     def total(terms):
         acc = terms[0].astype(F32)

time: 263 us -> 255 us (0.970)
  Pallas kernels: 262 us -> 255 us
    pallas_call x1, Pallas kernels: 249 us -> 242 us  [call(): pl.pallas_call(functools.partial(kernel, split, mats), out_shape=[pltpu.V...]
where the time goes in v3:
time: 255 us
  Pallas kernels  255 us (100%)
    pallas_call x1, Pallas kernels, call(): pl.pallas_call(functools.partial(kernel, split, mats), out_shape=[pltpu.V...  242 us
    pallas_call x1, Pallas kernels, call(): pl.pallas_call(flush, out_shape=[some((2, 2, 2, 4, 2, HALVES, high, 128),...  12.7 us

profile of v3, /device:TPU:0, one launch (start us, length us, event | category | flops | bytes accessed | tf_op | source)
XLA Modules:
  0.0 255.3 jit_solution(9130844989829153464)
XLA Ops:
  0.6 241.9 %step.1 = (bf16[12,2,2,4,352,128]{5,4,3,2,1,0:T(8,128)(2,1)S(1)}, bf16[12,2,2,4,352,128]{5,4,3,2,1,0:T(8,128)(2,1)S(1)}, f32[6,2,352,128]{3,2,1,0:T(8,128)S(1)}, f32[6,2,352,128]{3,2,1,0:T(8,128)S(1)}) custom-call(bf16[2,2,2,4,2,2,352,128]{7,6,5,4,3,2,1,0:T(8,128)(2,1)} %bitcast.105, bf16[2,2,2,4,2,2,352,128]{7,6,5,4,3,2,1,0:T(8,128)(2,1)} %bitcast.106, ...), custom_call_target="tpu_custom_call" | custom-call | tf_op jit(solution)/shard_map/step/pallas_call | solution.py:475
  242.6 12.7 %flush.1 = (bf16[2,2,2,4,2,2,352,128]{7,6,5,4,3,2,1,0:T(8,128)(2,1)}, bf16[2,2,2,4,2,2,352,128]{7,6,5,4,3,2,1,0:T(8,128)(2,1)}, bf16[2,2,2,4,2,2,352,128]{7,6,5,...) custom-call(bf16[12,2,2,4,352,128]{5,4,3,2,1,0:T(8,128)(2,1)S(1)} %g, ...), custom_call_target="tpu_custom_call" | custom-call | tf_op jit(solution)/shard_map/flush/pallas_call | solution.py:487
